TPU v7x, 32 devices: a whole 2x2x4 slice. The times are simulated.
32 devices in a mesh: freq: 8 (over z, x), sens: 4 (over y, core).
Axes of the slice: x: 2, y: 2, z: 4, core: 2. Of those that a mesh axis runs over, the one named last changes fastest.
Arguments:
- samples: bfloat16 [128, 608, 420], P('freq', 'sens'), may hold values from -6 to 6
- response_tiles: bfloat16 [448, 2, 608, 21], P('freq', None, 'sens'), may hold values from -0.25 to 0.25
- slot_sensor: int32 [608], P('sens'), may hold values from -1 to 599, as said below
- sensor_noise: float32 [600], replicated, may hold values from 0.02 to 5
- advance_offset: int32 [21], replicated, may hold values from 0 to 419
Outputs:
- outlook_values: bfloat16 [128, 21, 420], P('freq')
- noise_spread: float32 [21], replicated
Inputs may be any that keep to these rules, and one draw needn't show every extreme that they name: `slot_sensor`: every sensor number appears in exactly one slot; the other 8 slots hold -1.
All inputs are finite; a program needn't handle non-finite values.
Results may differ from a plain program's by a relative error of at most 0.0055.
Values may be sent and summed in bfloat16 or wider, within the bound.
A program may use at most 64 MiB of HBM per device.

v0:
```python
import math
import jax
import jax.numpy as jnp
from jax import lax
from jax.sharding import PartitionSpec as P

KEPT_HARMONICS = 448


def angles(first_bin, bin_count, period, factor):
    bin_index = first_bin + lax.iota(jnp.int32, bin_count)
    turn_count = bin_index[:, None] * factor[None, :] % period
    return turn_count.astype(jnp.float32) * (2.0 * math.pi / period)


def forward_table(bin_count, step_count, period):
    phase_angle = angles(0, bin_count, period, lax.iota(jnp.int32, step_count))
    return jnp.stack([jnp.cos(phase_angle), -jnp.sin(phase_angle)]).astype(jnp.bfloat16)


def inverse_table(bin_count, step_count, period):
    bin_index = lax.iota(jnp.int32, bin_count)
    weight = jnp.where(bin_index == 0, 1.0, 2.0).astype(jnp.float32) / period
    phase_angle = angles(0, bin_count, period, lax.iota(jnp.int32, step_count))
    return jnp.stack(
        [weight[:, None] * jnp.cos(phase_angle), -weight[:, None] * jnp.sin(phase_angle)]
    )


def contract(spectra, blocks):

    def product(left, right):
        return jnp.einsum("krs,ksq->kqr", left, right, preferred_element_type=jnp.float32)

    real_part = product(spectra[0], blocks[:, 0]) - product(spectra[1], blocks[:, 1])
    imag_part = product(spectra[0], blocks[:, 1]) + product(spectra[1], blocks[:, 0])
    return jnp.stack([real_part, imag_part])


def rotate(summed, first_bin, advance_offset, period):
    twiddle = angles(first_bin, summed.shape[1], period, advance_offset)[:, :, None]
    cosine = jnp.cos(twiddle)
    sine_part = jnp.sin(twiddle)
    real_part = summed[0] * cosine - summed[1] * sine_part
    imag_part = summed[0] * sine_part + summed[1] * cosine
    return jnp.stack([real_part, imag_part])


def on_device(samples, response_tiles, slot_sensor, sensor_noise, advance_offset):
    highest = lax.Precision.HIGHEST
    bins_dev = response_tiles.shape[0]
    first_bin = lax.axis_index("freq") * bins_dev
    period = 2 * KEPT_HARMONICS
    step_count = samples.shape[2]
    live_slot = (slot_sensor >= 0).astype(jnp.bfloat16)
    blocks = response_tiles * live_slot[None, None, :, None]
    sensor_ids = lax.iota(jnp.int32, sensor_noise.shape[0])
    slot_noise = jnp.sum(
        jnp.where(
            slot_sensor[:, None] == sensor_ids[None, :], sensor_noise[None, :], jnp.float32(0.0)
        ),
        axis=1,
    )
    wide = blocks.astype(jnp.float32)
    power = wide[:, 0] * wide[:, 0] + wide[:, 1] * wide[:, 1]
    bin_index = first_bin + lax.iota(jnp.int32, bins_dev)
    bin_weight = jnp.where(bin_index == 0, 1.0, 2.0).astype(jnp.float32) / period
    per_bin = jnp.einsum("ksq,s->kq", power, slot_noise, precision=highest)
    noise_spread = lax.psum(jnp.dot(bin_weight, per_bin, precision=highest), ("freq", "sens"))
    forward = forward_table(KEPT_HARMONICS, step_count, period)
    spectra = jnp.einsum(
        "rst,ckt->ckrs", samples, forward, preferred_element_type=jnp.float32
    ).astype(jnp.bfloat16)
    partial_value = contract(spectra, lax.all_gather(blocks, "freq", axis=0, tiled=True))
    base_bin = 0
    backward = inverse_table(KEPT_HARMONICS, step_count, period)
    summed = lax.psum(partial_value, "sens")
    shifted = rotate(summed, base_bin, advance_offset, period)
    kept_entries_local = jnp.einsum("ckqr,ckt->rqt", shifted, backward, precision=highest)
    outlook_values = kept_entries_local.astype(jnp.bfloat16)
    return (outlook_values, noise_spread)


def solution(mesh):
    placed = (P("freq", "sens", None), P("freq", None, "sens", None), P("sens"), P(), P())
    return jax.shard_map(
        on_device,
        mesh=mesh,
        in_specs=placed,
        out_specs=(P("freq", None, None), P()),
        check_vma=False,
    )
```

profile of v0, /device:TPU:0, one launch (start us, length us, event | category | flops | bytes accessed | tf_op | source)
XLA Modules:
  0.0 256.4 jit_solution(4376142394990606409)
XLA Ops:
  7.2 0.0 copy-start
  7.2 0.0 all-gather.2.cloned.1.call-start
  7.2 0.8 compare_convert_fusion
  8.1 0.0 copy-start.4
  8.1 0.0 copy-start.5
  8.1 3.6 %fusion.59 = (f32[56,2,152,21]{2,3,0,1:T(8,128)}, bf16[56,2,152,21]{2,3,0,1:T(8,128)(2,1)}) fusion(bf16[152]{0:T(256)(128)(2,1)S(1)} %compare_convert_fusion, bf16[56,2,152,21]{2,1,3,0:T(2,128)(2,1)} %param.6), kind=kLoop, calls=%fused_computation.80 | loop fusion | flops 715008 | bytes 2860336 | tf_op jit(solution)/shard_map/convert_element_type | solution.py:64
  11.7 0.0 all-gather.2.cloned.1.call-update
  11.7 0.0 all-reduce.2.cloned.1.call-start
  11.8 0.0 copy-done.4
  11.8 0.0 copy-done.5
  11.8 0.2 select_reduce_fusion
  12.0 1.9 fusion.10
  13.9 1.9 fusion.17
  15.8 0.1 copy.35
  15.9 0.1 convolution_bitcast_fusion
  16.1 45.9 %psum.15 = f32[21]{0:T(128)} all-reduce(f32[21]{0:T(128)S(1)} %convolution_bitcast_fusion), channel_id=1, replica_groups=mesh['freq'=8,'sens'=4] {'freq','sens'}, use_global_device_ids=true, to_apply=%region_2.3 | all-reduce | flops 21 | bytes 168 | tf_op jit(solution)/shard_map/psum | solution.py:69
  62.0 3.8 %negate_convert_fusion = (bf16[1,448,420]{1,2,0:T(8,128)(2,1)S(1)}, bf16[1,448,420]{1,2,0:T(8,128)(2,1)S(1)}) fusion(), kind=kLoop, calls=%fused_computation.36 | loop fusion | flops 2257920 | bytes 752640 | tf_op jit(solution)/shard_map/convert.1
  65.8 0.0 copy-done
  65.8 2.9 %convolution_convert_fusion = bf16[2,448,16,152]{1,3,2,0:T(8,128)(2,1)S(1)} fusion(bf16[16,152,420]{2,1,0:T(8,128)(2,1)S(1)} %copy-done, bf16[1,448,420]{1,2,0:T(8,128)(2,1)S(1)} %get-tuple-element.16, bf16[1,448,420]{1,2,0:T(8,128)(2,1)S(1)} %get-tuple-element.17), kind=kOutput, calls=%fused_computation.8 | convolution fusion | flops 1834104832 | bytes 7153664 | tf_op jit(solution)/shard_map/rst,ckt->ckrs/dot_general | solution.py:71
  68.7 2.6 %slice_bitcast_fusion.7 = (bf16[448,16,152]{0,2,1:T(8,128)(2,1)}, bf16[448,16,152]{0,2,1:T(8,128)(2,1)}) fusion(bf16[2,448,16,152]{1,3,2,0:T(8,128)(2,1)S(1)} %convolution_convert_fusion), kind=kLoop, calls=%fused_computation.10 | loop fusion | bytes 8716288 | tf_op jit(solution)/shard_map/squeeze | solution.py:35
  71.3 7.4 %copy.24 = bf16[448,16,152]{2,1,0:T(8,128)(2,1)} copy(bf16[448,16,152]{0,2,1:T(8,128)(2,1)} %get-tuple-element.8) | data formatting | bytes 4358144 | tf_op jit(solution)/shard_map/squeeze | solution.py:35
  78.8 7.5 %copy.25 = bf16[448,16,152]{2,1,0:T(8,128)(2,1)} copy(bf16[448,16,152]{0,2,1:T(8,128)(2,1)} %get-tuple-element.9) | data formatting | bytes 4358144 | tf_op jit(solution)/shard_map/squeeze | solution.py:35
  86.3 86.1 %all-gather.2.cloned.1.call-done = bf16[448,2,152,21]{2,3,0,1:T(8,128)(2,1)} async-done(((bf16[56,2,152,21]{2,3,0,1:T(8,128)(2,1)}), bf16[448,2,152,21]{2,3,0,1:T(8,128)(2,1)}) %all-gather.2.cloned.1.call-update) | async-done | bytes 5720080 | tf_op jit(solution)/shard_map/all_gather | solution.py:74
  172.4 0.0 copy-start.1
  172.4 5.3 %fusion = f32[448,21,16]{1,2,0:T(8,128)S(1)} fusion(bf16[448,16,152]{2,1,0:T(8,128)(2,1)} %copy.25, bf16[448,2,152,21]{2,3,0,1:T(8,128)(2,1)} %all-gather.2.cloned.1.call-done), kind=kOutput, calls=%fused_computation.2 | convolution fusion | flops 45760512 | bytes 9777152 | tf_op jit(solution)/shard_map/krs,ksq->kqr/dot_general | solution.py:33
  177.8 1.4 copy-done.1
  179.2 5.5 %add_bitcast_fusion = f32[1,448,21,16]{2,3,1,0:T(8,128)} fusion(f32[448,21,16]{1,2,0:T(8,128)S(1)} %fusion, bf16[448,16,152]{2,1,0:T(8,128)(2,1)} %copy.24, bf16[448,2,152,21]{2,3,0,1:T(8,128)(2,1)S(1)} %copy-done.1), kind=kOutput, calls=%fused_computation.6 | convolution fusion | flops 45911040 | bytes 11956224 | tf_op jit(solution)/shard_map/krs,ksq->kqr/dot_general | solution.py:33
  184.7 3.0 %copy.29 = f32[1,448,21,16]{1,3,2,0:T(8,128)S(1)} copy(f32[1,448,21,16]{2,3,1,0:T(8,128)} %add_bitcast_fusion) | data formatting | bytes 1204224 | tf_op jit(solution)/shard_map/stack | solution.py:37
  187.7 0.0 copy-start.2
  187.7 5.3 %fusion.1 = f32[448,21,16]{1,2,0:T(8,128)S(1)} fusion(bf16[448,16,152]{2,1,0:T(8,128)(2,1)} %copy.24, bf16[448,2,152,21]{2,3,0,1:T(8,128)(2,1)} %all-gather.2.cloned.1.call-done), kind=kOutput, calls=%fused_computation.3 | convolution fusion | flops 45760512 | bytes 9777152 | tf_op jit(solution)/shard_map/krs,ksq->kqr/dot_general | solution.py:33
  193.0 0.0 copy-done.2
  193.0 6.1 %subtract_bitcast_fusion = f32[1,448,21,16]{2,3,1,0:T(8,128)} fusion(f32[448,21,16]{1,2,0:T(8,128)S(1)} %fusion.1, bf16[448,16,152]{2,1,0:T(8,128)(2,1)S(1)} %copy-done.2, bf16[448,2,152,21]{2,3,0,1:T(8,128)(2,1)} %all-gather.2.cloned.1.call-done), kind=kOutput, calls=%fused_computation.7 | convolution fusion | flops 45911040 | bytes 8888320 | tf_op jit(solution)/shard_map/krs,ksq->kqr/dot_general | solution.py:33
  199.2 3.7 %copy.28 = f32[1,448,21,16]{1,3,2,0:T(8,128)} copy(f32[1,448,21,16]{2,3,1,0:T(8,128)} %subtract_bitcast_fusion) | data formatting | bytes 1204224 | tf_op jit(solution)/shard_map/stack | solution.py:37
  202.8 0.0 copy-start.6
  202.8 2.4 pad_maximum_fusion
  205.2 0.0 all-reduce.2.cloned.1.call-update
  205.2 0.0 copy-done.6
  205.2 0.3 fusion.39
  205.5 4.5 %fusion.31 = (f32[1,448,420]{1,2,0:T(8,128)S(1)}, f32[1,448,420]{1,2,0:T(8,128)}) fusion(f32[448]{0:T(512)S(1)} %select_multiply_fusion, f32[448]{0:T(512)S(1)} %fusion.42), kind=kLoop, calls=%fused_computation.43 | loop fusion | flops 2069760 | bytes 1508864 | tf_op jit(solution)/shard_map/mul | solution.py:26
  210.0 33.6 %all-reduce.2.cloned.1.call-done = f32[2,448,21,16]{1,3,2,0:T(8,128)} async-done(((f32[2,448,21,16]{1,3,2,0:T(8,128)}), f32[2,448,21,16]{1,3,2,0:T(8,128)}) %all-reduce.2.cloned.1.call-update) | async-done | bytes 1204240 | tf_op jit(solution)/shard_map/psum | solution.py:77
  243.6 0.0 copy-start.3
  243.6 1.6 multiply_subtract_fusion
  245.2 0.1 pad_maximum_fusion.1
  245.3 0.0 copy-done.3
  245.3 3.4 %fusion.19 = bf16[16,21,420]{2,1,0:T(8,128)(2,1)S(1)} fusion(f32[2,448,21,16]{1,3,2,0:T(8,128)S(1)} %pad_maximum_fusion.1, f32[1,448,420]{1,2,0:T(8,128)S(1)} %copy-done.3, f32[1,448,420]{1,2,0:T(8,128)S(1)} %get-tuple-element.18), kind=kOutput, calls=%fused_computation.29 | convolution fusion | flops 1517839616 | bytes 2991744 | tf_op jit(solution)/shard_map/ckqr,ckt->rqt/dot_general | solution.py:79
  248.7 0.8 copy.31
  (2 shorter events, 0.0 us)
Async XLA Ops:
  7.2 58.6 %copy-start = (bf16[16,152,420]{2,1,0:T(8,128)(2,1)S(1)}, bf16[16,152,420]{2,1,0:T(8,128)(2,1)}, u32[]{:S(2)}) copy-start(bf16[16,152,420]{2,1,0:T(8,128)(2,1)} %param.5) | copy-start | bytes 6128644
  7.2 165.2 %all-gather.2.cloned.1.call-start = ((), (), s32[]{:S(2)}) async-start(), calls=%async_computation | async-start | bytes 12386304 | tf_op jit(solution)/shard_map/all_gather | solution.py:74
  8.1 3.7 %copy-start.4 = (f32[600]{0:T(1024)S(1)}, f32[600]{0:T(1024)}, u32[]{:S(2)}) copy-start(f32[600]{0:T(1024)} %param.8) | copy-start | bytes 7204
  8.1 3.7 %copy-start.5 = (s32[152]{0:T(256)S(1)}, s32[152]{0:T(256)}, u32[]{:S(2)}) copy-start(s32[152]{0:T(256)} %param.7) | copy-start | bytes 1828
  11.7 231.8 %all-reduce.2.cloned.1.call-start = ((), (), s32[]{:S(2)}) async-start(), calls=%async_computation.1 | async-start | bytes 2752512 | tf_op jit(solution)/shard_map/psum | solution.py:77
  172.4 6.8 %copy-start.1 = (bf16[448,2,152,21]{2,3,0,1:T(8,128)(2,1)S(1)}, bf16[448,2,152,21]{2,3,0,1:T(8,128)(2,1)}, u32[]{:S(2)}) copy-start(bf16[448,2,152,21]{2,3,0,1:T(8,128)(2,1)} %all-gather.2.cloned.1.call-done) | copy-start | bytes 17160196
  187.7 5.4 %copy-start.2 = (bf16[448,16,152]{2,1,0:T(8,128)(2,1)S(1)}, bf16[448,16,152]{2,1,0:T(8,128)(2,1)}, u32[]{:S(2)}) copy-start(bf16[448,16,152]{2,1,0:T(8,128)(2,1)} %copy.25) | copy-start | bytes 6537220
  202.8 2.4 copy-start.6
  243.6 1.7 copy-start.3
Sparse Core Ops, SparseCore 0:
  11.9 160.5 all-gather.1
  205.3 38.1 all-reduce.1
where the time goes:
time: 257 us; the launch traced here: 256 us
  waiting for transfers between devices  120 us (47%)
  blocking collectives  45.9 us (18%)
  matrix products  30.6 us (12%)
  local copies, waits for them, and re-layouts  26.6 us (10%)
  other arithmetic  19.2 us (7%)
  between operations  14.2 us (6%)
    all_gather x1, waiting for transfers between devices, on_device(): lax.all_gather(blocks, 'freq', axis=0, tiled=True)  86.1 us
    psum x1, blocking collectives, on_device(): lax.psum(jnp.dot(bin_weight, per_bin, precision=highest), ('freq', 'sens'))  45.9 us
    psum x1, waiting for transfers between devices, on_device(): summed = lax.psum(partial_value, 'sens')  33.6 us
    dot_general x4, matrix products, product(): jnp.einsum('krs,ksq->kqr', left, right, preferred_element_type=jnp.float32)  22.3 us
    squeeze x2, local copies, waits for them, and re-layouts, contract(): spectra[0]  10 us
    squeeze x1, local copies, waits for them, and re-layouts, contract(): spectra[1]  7.52 us
    another operation x2, local copies, waits for them, and re-layouts, contract(): return jnp.stack([real_part, imag_part])  6.64 us
  transfers between devices with their start and end apart: 2, of which 2 were waited for; matrix products, arithmetic and copies ran while one was open for 13% of the time, Pallas kernels for 0%

commit v1 on v0

--- a/solution.py
+++ b/solution.py
@@ -71,7 +71,18 @@
     spectra = jnp.einsum(
         "rst,ckt->ckrs", samples, forward, preferred_element_type=jnp.float32
     ).astype(jnp.bfloat16)
-    partial_value = contract(spectra, lax.all_gather(blocks, "freq", axis=0, tiled=True))
+    partial_value = contract(
+        spectra,
+        jnp.concatenate(
+            lax.all_to_all(
+                jnp.stack([blocks for _ in range(lax.axis_size("freq"))], axis=0),
+                axis_name="freq",
+                concat_axis=0,
+                split_axis=0,
+            ),
+            0,
+        ),
+    )
     base_bin = 0
     backward = inverse_table(KEPT_HARMONICS, step_count, period)
     summed = lax.psum(partial_value, "sens")

time: 257 us -> 363 us (1.41)
  blocking collectives: 45.9 us -> 226 us
  waiting for transfers between devices: 120 us -> 35.2 us
  local copies, waits for them, and re-layouts: 26.6 us -> 35.9 us
  starting transfers between devices: 0.08 us -> 7.45 us
    psum x1, blocking collectives: 45.9 us -> 226 us  [on_device(): lax.psum(jnp.dot(bin_weight, per_bin, precision=highest), ('freq', 'sens'))]
    all_gather x1 -> x0, waiting for transfers between devices: 86.1 us -> none  [on_device(): lax.all_gather(blocks, 'freq', axis=0, tiled=True)]
    all_to_all x0 -> x1, starting transfers between devices: none -> 7.41 us  [on_device(): lax.all_to_all(jnp.stack([blocks for _ in range(lax.axis_size('freq'))],...]
    all_to_all x0 -> x1, local copies, waits for them, and re-layouts: none -> 7.12 us  [on_device(): lax.all_to_all(jnp.stack([blocks for _ in range(lax.axis_size('freq'))],...]
    another operation x0 -> x1, local copies, waits for them, and re-layouts: none -> 4.3 us  [on_device(): jnp.stack([blocks for _ in range(lax.axis_size('freq'))], axis=0)]
    dot_general x4, matrix products: 22.3 us -> 18.4 us  [product(): jnp.einsum('krs,ksq->kqr', left, right, preferred_element_type=jnp.float32)]
  transfers between devices with their start and end apart: 2 -> 2, of which waited for: 2 -> 1; matrix products, arithmetic and copies ran while one was open for 13% -> 8% of each run, Pallas kernels for 0% -> 0%
where the time goes in v1:
time: 363 us
  blocking collectives  226 us (62%)
  local copies, waits for them, and re-layouts  35.9 us (10%)
  waiting for transfers between devices  35.2 us (10%)
  matrix products  28.2 us (8%)
  other arithmetic  15.7 us (4%)
  between operations  14.2 us (4%)
  starting transfers between devices  7.45 us (2%)
    psum x1, blocking collectives, on_device(): lax.psum(jnp.dot(bin_weight, per_bin, precision=highest), ('freq', 'sens'))  226 us
    psum x1, waiting for transfers between devices, on_device(): summed = lax.psum(partial_value, 'sens')  35.2 us
    dot_general x4, matrix products, product(): jnp.einsum('krs,ksq->kqr', left, right, preferred_element_type=jnp.float32)  18.4 us
    squeeze x2, local copies, waits for them, and re-layouts, contract(): spectra[0]  9.33 us
    all_to_all x1, starting transfers between devices, on_device(): lax.all_to_all(jnp.stack([blocks for _ in range(lax.axis_size('freq'))],...  7.41 us
  transfers between devices with their start and end apart: 2, of which 1 were waited for; matrix products, arithmetic and copies ran while one was open for 8% of the time, Pallas kernels for 0%

profile of v1, /device:TPU:0, one launch (start us, length us, event | category | flops | bytes accessed | tf_op | source)
XLA Modules:
  0.0 362.8 jit_solution(15439174408532347498)
XLA Ops:
  7.2 0.0 copy-start
  7.2 0.8 compare_convert_fusion
  8.0 3.0 fusion.59
  11.0 4.3 %stack.16 = bf16[8,56,2,152,21]{3,1,4,2,0:T(8,128)(2,1)} broadcast(bf16[56,2,152,21]{2,0,3,1:T(8,128)(2,1)S(1)} %get-tuple-element.11), dimensions={1,2,3,4} | broadcast | bytes 6435072 | tf_op jit(solution)/shard_map/stack | solution.py:78
  15.3 0.0 copy-start.7
  15.3 0.0 copy-start.8
  15.3 7.4 %all-to-all-start = ((bf16[8,56,2,152,21]{3,1,4,2,0:T(8,128)(2,1)}), bf16[8,56,2,152,21]{3,1,4,2,0:T(8,128)(2,1)}, u32[]{:S(2)}, u32[]{:S(2)}) async-start(bf16[8,56,2,152,21]{3,1,4,2,0:T(8,128)(2,1)} %stack.16), calls=%async_computation | async-start | bytes 19267584 | tf_op jit(solution)/shard_map/all_to_all | solution.py:77
  22.7 0.0 all-reduce.2.cloned.1.call-start
  22.7 0.0 copy-done.7
  22.8 0.0 copy-done.8
  22.8 0.2 select_reduce_fusion
  23.0 3.4 fusion.17
  26.3 0.1 copy.44
  26.4 0.1 convolution_bitcast_fusion
  26.6 226.2 %psum.15 = f32[21]{0:T(128)} all-reduce(f32[21]{0:T(128)S(1)} %convolution_bitcast_fusion), channel_id=1, replica_groups=mesh['freq'=8,'sens'=4] {'freq','sens'}, use_global_device_ids=true, to_apply=%region_2.3 | all-reduce | flops 21 | bytes 168 | tf_op jit(solution)/shard_map/psum | solution.py:69
  252.7 3.8 %negate_convert_fusion = (bf16[1,448,420]{1,2,0:T(8,128)(2,1)S(1)}, bf16[1,448,420]{1,2,0:T(8,128)(2,1)S(1)}) fusion(), kind=kLoop, calls=%fused_computation.35 | loop fusion | flops 2257920 | bytes 752640 | tf_op jit(solution)/shard_map/convert.1
  256.5 0.0 copy-done
  256.5 2.9 convolution_convert_fusion
  259.5 1.9 slice_bitcast_fusion.7
  261.3 7.4 %copy.34 = bf16[448,16,152]{2,1,0:T(8,128)(2,1)} copy(bf16[448,16,152]{0,2,1:T(8,128)(2,1)} %get-tuple-element.12) | data formatting | bytes 4358144 | tf_op jit(solution)/shard_map/squeeze | solution.py:35
  268.8 5.5 %copy.35 = bf16[448,16,152]{2,1,0:T(8,128)(2,1)} copy(bf16[448,16,152]{0,2,1:T(8,128)(2,1)S(1)} %get-tuple-element.13) | data formatting | bytes 4358144 | tf_op jit(solution)/shard_map/squeeze | solution.py:35
  274.3 0.0 all-to-all-done
  274.3 0.0 copy-start.3
  274.3 7.1 %copy.33 = bf16[8,56,2,152,21]{3,4,1,0,2:T(8,128)(2,1)S(1)} copy(bf16[8,56,2,152,21]{3,1,4,2,0:T(8,128)(2,1)} %all-to-all-done) | data formatting | bytes 11440128 | tf_op jit(solution)/shard_map/all_to_all | solution.py:77
  281.4 0.0 copy-start.2
  281.4 0.0 copy-done.3
  281.4 0.0 copy-start.4
  281.5 3.4 fusion.1
  284.8 1.3 copy-done.4
  286.2 0.0 copy-start.5
  286.2 3.4 fusion
  289.6 0.5 copy-done.2
  290.1 0.9 copy-done.5
  291.0 3.4 subtract_bitcast_fusion
  294.3 3.0 copy.38
  297.3 8.2 %add_bitcast_fusion = f32[1,448,21,16]{2,3,1,0:T(8,128)} fusion(f32[448,21,16]{1,2,0:T(8,128)} %fusion, bf16[448,16,152]{2,1,0:T(8,128)(2,1)} %copy.34, bf16[448,2,152,21]{2,3,0,1:T(8,128)(2,1)} %bitcast.67), kind=kOutput, calls=%fused_computation.6 | convolution fusion | flops 45911040 | bytes 13447168 | tf_op jit(solution)/shard_map/krs,ksq->kqr/dot_general | solution.py:33
  305.5 0.0 copy-start.9
  305.5 3.0 copy.39
  308.5 1.3 pad_maximum_fusion
  309.8 0.0 all-reduce.2.cloned.1.call-update
  309.8 0.0 copy-done.9
  309.8 0.3 fusion.39
  310.1 4.7 %fusion.31 = (f32[1,448,420]{1,2,0:T(8,128)S(1)}, f32[1,448,420]{1,2,0:T(8,128)}) fusion(f32[448]{0:T(512)S(1)} %select_multiply_fusion, f32[448]{0:T(512)S(1)} %fusion.42), kind=kLoop, calls=%fused_computation.42 | loop fusion | flops 2069760 | bytes 1508864 | tf_op jit(solution)/shard_map/mul | solution.py:26
  314.8 35.2 %all-reduce.2.cloned.1.call-done = f32[2,448,21,16]{1,3,2,0:T(8,128)} async-done(((f32[2,448,21,16]{1,3,2,0:T(8,128)}), f32[2,448,21,16]{1,3,2,0:T(8,128)}) %all-reduce.2.cloned.1.call-update) | async-done | bytes 1204240 | tf_op jit(solution)/shard_map/psum | solution.py:88
  350.0 0.0 copy-start.6
  350.0 1.6 multiply_subtract_fusion
  351.5 0.0 copy-start.1
  351.6 0.1 pad_maximum_fusion.1
  351.7 0.0 copy-done.6
  351.7 3.4 fusion.19
  355.1 0.8 copy.41
  355.9 0.0 copy-done.1
  (2 shorter events, 0.0 us)
Async XLA Ops:
  7.2 249.3 %copy-start = (bf16[16,152,420]{2,1,0:T(8,128)(2,1)S(1)}, bf16[16,152,420]{2,1,0:T(8,128)(2,1)}, u32[]{:S(2)}) copy-start(bf16[16,152,420]{2,1,0:T(8,128)(2,1)} %param.5) | copy-start | bytes 6128644
  15.3 7.5 %copy-start.7 = (f32[600]{0:T(1024)S(1)}, f32[600]{0:T(1024)}, u32[]{:S(2)}) copy-start(f32[600]{0:T(1024)} %param.8) | copy-start | bytes 7204
  15.3 7.5 %copy-start.8 = (s32[152]{0:T(256)S(1)}, s32[152]{0:T(256)}, u32[]{:S(2)}) copy-start(s32[152]{0:T(256)} %param.7) | copy-start | bytes 1828
  15.3 259.0 %all-to-all-start = ((bf16[8,56,2,152,21]{3,1,4,2,0:T(8,128)(2,1)}), bf16[8,56,2,152,21]{3,1,4,2,0:T(8,128)(2,1)}, u32[]{:S(2)}, u32[]{:S(2)}) async-start(bf16[8,56,2,152,21]{3,1,4,2,0:T(8,128)(2,1)} %stack.16), calls=%async_computation | async-start | bytes 19267584 | tf_op jit(solution)/shard_map/all_to_all | solution.py:77
  22.7 327.3 %all-reduce.2.cloned.1.call-start = ((), (), s32[]{:S(2)}) async-start(), calls=%async_computation.1 | async-start | bytes 2752512 | tf_op jit(solution)/shard_map/psum | solution.py:88
  274.3 7.1 %copy-start.3 = (bf16[448,16,152]{2,1,0:T(8,128)(2,1)S(1)}, bf16[448,16,152]{2,1,0:T(8,128)(2,1)}, u32[]{:S(2)}) copy-start(bf16[448,16,152]{2,1,0:T(8,128)(2,1)} %copy.34) | copy-start | bytes 6537220
  281.4 8.7 %copy-start.2 = (bf16[8,56,2,152,21]{3,4,1,0,2:T(8,128)(2,1)}, bf16[8,56,2,152,21]{3,4,1,0,2:T(8,128)(2,1)S(1)}, u32[]{:S(2)}) copy-start(bf16[8,56,2,152,21]{3,4,1,0,2:T(8,128)(2,1)S(1)} %copy.33) | copy-start | bytes 17160196
  281.4 4.7 %copy-start.4 = (bf16[448,16,152]{2,1,0:T(8,128)(2,1)S(1)}, bf16[448,16,152]{2,1,0:T(8,128)(2,1)}, u32[]{:S(2)}) copy-start(bf16[448,16,152]{2,1,0:T(8,128)(2,1)} %copy.35) | copy-start | bytes 6537220
  286.2 4.8 %copy-start.5 = (f32[448,21,16]{1,2,0:T(8,128)S(1)}, f32[448,21,16]{1,2,0:T(8,128)}, u32[]{:S(2)}) copy-start(f32[448,21,16]{1,2,0:T(8,128)} %fusion.1) | copy-start | bytes 1806340
  305.5 4.3 %copy-start.9 = (s32[21]{0:T(128)S(1)}, s32[21]{0:T(128)}, u32[]{:S(2)}) copy-start(s32[21]{0:T(128)} %param.9) | copy-start | bytes 256
  350.0 1.7 copy-start.6
  351.5 4.4 %copy-start.1 = (bf16[16,152,420]{2,1,0:T(8,128)(2,1)S(1)}, bf16[16,152,420]{2,1,0:T(8,128)(2,1)}, u32[]{:S(2)}) copy-start(bf16[16,152,420]{2,1,0:T(8,128)(2,1)} %param.5) | copy-start | bytes 6128644
Sparse Core Ops, SparseCore 0:
  309.9 39.9 all-reduce.1
